TPU v7x, 8 devices: a whole 2x2x1 slice. The times are simulated.
8 devices in a mesh: dp: 2 (over z, y), tp: 4 (over x, core).
Axes of the slice: x: 2, y: 2, z: 1, core: 2. Of those that a mesh axis runs over, the one named last changes fastest.
Arguments:
- x_tokens: bfloat16 [12, 64, 4096], P('dp', 'tp'), parts along dimension 0
- start_pos: int32 [12], P('dp'), parts along dimension 0
- k_cache: bfloat16 [2, 12, 8, 3136, 128], P(None, 'dp', 'tp'), parts along dimension 1
- v_cache: bfloat16 [2, 12, 8, 3136, 128], P(None, 'dp', 'tp'), parts along dimension 1
- w_q: bfloat16 [2, 4096, 6144], P(None, None, 'tp')
- w_k: bfloat16 [2, 4096, 1024], P(None, None, 'tp')
- w_v: bfloat16 [2, 4096, 1024], P(None, None, 'tp')
- w_o: bfloat16 [2, 6144, 4096], P(None, 'tp')
- w_up: bfloat16 [2, 4096, 16384], P(None, None, 'tp')
- w_down: bfloat16 [2, 16384, 4096], P(None, 'tp')
- ln_gain: bfloat16 [2, 2, 4096], replicated
- ln_bias: bfloat16 [2, 2, 4096], replicated
Outputs:
- output 1: bfloat16 [12, 64, 4096], P('dp', 'tp'), parts along dimension 0
- output 2: bfloat16 [2, 12, 8, 3136, 128], P(None, 'dp', 'tp'), parts along dimension 1
- output 3: bfloat16 [2, 12, 8, 3136, 128], P(None, 'dp', 'tp'), parts along dimension 1
There are 2 independent parts. A program takes and returns all parts, laid end to end along the dimension named above; an argument that names none is the same for every part.
All inputs are finite; a program needn't handle non-finite values.
Results may differ from a plain program's by a relative error of at most 0.0189325.
Values are sent between devices in bfloat16 or wider.
A program may use at most 1.25 GiB of HBM per device.

v0:
```python
import jax
import jax.numpy as jnp
from jax import lax
from jax.sharding import PartitionSpec as P

LN_EPS = 1e-5
ROPE_BASE = 10000.0
NEG_BIG = -1e30


def layer_norm1p(values_in, gain, bias):
    x_float = values_in.astype(jnp.float32)
    row_mean = jnp.mean(x_float, axis=-1, keepdims=True)
    centered = x_float - row_mean
    variance = jnp.mean(centered * centered, axis=-1, keepdims=True)
    normed = centered * lax.rsqrt(variance + LN_EPS)
    return (normed * (1.0 + gain.astype(jnp.float32)) + bias.astype(jnp.float32)).astype(jnp.bfloat16)


def rotate_half(values_in, positions):
    rot_dim = values_in.shape[-1] // 2
    half_rot = rot_dim // 2
    inv_freq = ROPE_BASE ** (-(jnp.arange(half_rot, dtype=jnp.float32) * (2.0 / rot_dim)))
    angles = positions.astype(jnp.float32)[..., None] * inv_freq
    cos_a = jnp.cos(angles)
    sin_a = jnp.sin(angles)
    first = values_in[..., :half_rot]
    second = values_in[..., half_rot:rot_dim]
    return jnp.concatenate([first * cos_a - second * sin_a, second * cos_a + first * sin_a, values_in[..., rot_dim:]], axis=-1)


def write_rows(cache_seq, new_rows, start_row):
    zero_idx = jnp.zeros_like(start_row)
    return lax.dynamic_update_slice(cache_seq, new_rows, (zero_idx, start_row, zero_idx))


def attention(q_rot, k_all, v_all, key_ok, scale):
    scores = jnp.einsum('bkgch,bksh->bkgcs', q_rot, k_all, preferred_element_type=jnp.float32) * scale
    scores = jnp.where(key_ok, scores, NEG_BIG)
    peak = jnp.max(scores, axis=-1, keepdims=True)
    weights = jnp.exp(scores - peak)
    row_sum = jnp.sum(weights, axis=-1, keepdims=True)
    context = jnp.einsum('bkgcs,bksh->bkgch', weights.astype(jnp.bfloat16), v_all, preferred_element_type=jnp.float32) / row_sum
    return context.astype(jnp.bfloat16)


def solution(mesh):
    tp_size = mesh.shape['tp']
    tok_spec = P('dp', 'tp', None)
    cache_spec = P(None, 'dp', 'tp', None, None)
    col_spec = P(None, None, 'tp')
    row_spec = P(None, 'tp', None)

    def device_fn(x_loc, start_pos, k_cache, v_cache, w_q, w_k, w_v, w_o, w_up, w_down, ln_gain, ln_bias):
        n_layers = w_q.shape[0]
        tok_loc = x_loc.shape[1]
        d_model = x_loc.shape[2]
        kv_loc = k_cache.shape[2]
        cache_len = k_cache.shape[3]
        head_dim = k_cache.shape[4]
        group_size = w_q.shape[2] // head_dim // kv_loc
        new_len = tok_loc * tp_size
        scale = head_dim ** -0.5
        positions = start_pos[:, None] + jnp.arange(new_len, dtype=jnp.int32)[None, :]
        key_ok = jnp.arange(cache_len, dtype=jnp.int32)[None, None, None, None, :] <= positions[:, None, None, :, None]
        hidden = x_loc
        k_list = []
        v_list = []
        for layer in range(n_layers):
            normed = layer_norm1p(hidden, ln_gain[layer, 0], ln_bias[layer, 0])
            normed_all = lax.all_gather(normed, 'tp', axis=1, tiled=True)
            q_proj = jnp.einsum('bcd,dkgh->bkgch', normed_all, w_q[layer].reshape(d_model, kv_loc, group_size, head_dim), preferred_element_type=jnp.float32)
            k_proj = jnp.einsum('bcd,dkh->bkch', normed_all, w_k[layer].reshape(d_model, kv_loc, head_dim), preferred_element_type=jnp.float32)
            v_rows = jnp.einsum('bcd,dkh->bkch', normed_all, w_v[layer].reshape(d_model, kv_loc, head_dim), preferred_element_type=jnp.float32).astype(jnp.bfloat16)
            q_rot = rotate_half(q_proj, positions[:, None, None, :]).astype(jnp.bfloat16)
            k_rows = rotate_half(k_proj, positions[:, None, :]).astype(jnp.bfloat16)
            k_new = jax.vmap(write_rows)(k_cache[layer], k_rows, start_pos)
            v_new = jax.vmap(write_rows)(v_cache[layer], v_rows, start_pos)
            context = attention(q_rot, k_new, v_new, key_ok, scale)
            attn_part = jnp.einsum('bkgch,kghd->bcd', context, w_o[layer].reshape(kv_loc, group_size, head_dim, d_model), preferred_element_type=jnp.float32).astype(jnp.bfloat16)
            attn_loc = lax.psum_scatter(attn_part, 'tp', scatter_dimension=1, tiled=True)
            after_attn = (hidden.astype(jnp.float32) + attn_loc.astype(jnp.float32)).astype(jnp.bfloat16)
            normed_mlp = layer_norm1p(after_attn, ln_gain[layer, 1], ln_bias[layer, 1])
            normed_mlp_all = lax.all_gather(normed_mlp, 'tp', axis=1, tiled=True)
            up_val = jnp.einsum('bcd,df->bcf', normed_mlp_all, w_up[layer], preferred_element_type=jnp.float32)
            act_sq = jnp.square(jnp.maximum(up_val, 0.0)).astype(jnp.bfloat16)
            mlp_part = jnp.einsum('bcf,fd->bcd', act_sq, w_down[layer], preferred_element_type=jnp.float32).astype(jnp.bfloat16)
            mlp_loc = lax.psum_scatter(mlp_part, 'tp', scatter_dimension=1, tiled=True)
            hidden = (after_attn.astype(jnp.float32) + mlp_loc.astype(jnp.float32)).astype(jnp.bfloat16)
            k_list.append(k_new)
            v_list.append(v_new)
        return hidden, jnp.stack(k_list), jnp.stack(v_list)

    return jax.shard_map(device_fn, mesh=mesh, in_specs=(tok_spec, P('dp'), cache_spec, cache_spec, col_spec, col_spec, col_spec, row_spec, col_spec, row_spec, P(), P()), out_specs=(tok_spec, cache_spec, cache_spec), check_vma=False)
```

profile of v0, /device:TPU:0, one launch (start us, length us, event | category | flops | bytes accessed | tf_op | source)
XLA Modules:
  0.0 787.2 jit_solution(16431752782436596484)
XLA Ops:
  15.5 15.1 %slice_bitcast_fusion.2 = (bf16[6,2,3136,128]{3,2,1,0:T(8,128)(2,1)}, bf16[6,2,3136,128]{3,2,1,0:T(8,128)(2,1)}) fusion(bf16[2,6,2,3136,128]{4,3,2,1,0:T(8,128)(2,1)} %param.15), kind=kLoop, calls=%fused_computation.58 | loop fusion | bytes 38535168 | tf_op jit(solution)/shard_map/squeeze | solution.py:78
  43.6 17.1 %fusion.152 = (bf16[1,4096,1536]{2,1,0:T(8,128)(2,1)}, bf16[1,4096,1536]{2,1,0:T(8,128)(2,1)}) fusion(bf16[2,4096,1536]{2,1,0:T(8,128)(2,1)} %param.16), kind=kLoop, calls=%fused_computation.181 | loop fusion | bytes 50331648 | tf_op jit(solution)/shard_map/slice | solution.py:72
  60.7 16.7 %copy.77 = bf16[1,4096,1536]{1,2,0:T(8,128)(2,1)} copy(bf16[1,4096,1536]{2,1,0:T(8,128)(2,1)} %get-tuple-element.96) | data formatting | bytes 25165824
  78.3 14.9 %slice_bitcast_fusion.1 = (bf16[6,2,3136,128]{3,2,1,0:T(8,128)(2,1)}, bf16[6,2,3136,128]{3,2,1,0:T(8,128)(2,1)}) fusion(bf16[2,6,2,3136,128]{4,3,2,1,0:T(8,128)(2,1)} %param.14), kind=kLoop, calls=%fused_computation.57 | loop fusion | bytes 38535168 | tf_op jit(solution)/shard_map/squeeze | solution.py:77
  93.2 17.7 %fusion.151 = (bf16[1,1536,4096]{2,1,0:T(8,128)(2,1)}, bf16[1,1536,4096]{2,1,0:T(8,128)(2,1)}) fusion(bf16[2,1536,4096]{2,1,0:T(8,128)(2,1)} %param.19), kind=kLoop, calls=%fused_computation.180 | loop fusion | bytes 50331648 | tf_op jit(solution)/shard_map/slice | solution.py:80
  127.7 57.1 %while.5 = (s32[]{:T(128)}, bf16[6,2,3136,128]{3,2,1,0:T(8,128)(2,1)}, s32[6,4]{0,1:T(4,128)S(1)}, bf16[6,2,64,128]{3,2,1,0:T(8,128)(2,1)}, s32[]{:T(128)}, /*index=5*/s32[4]{0:T(128)S(1)}, s32[]{:T(128)}) while((s32[]{:T(128)}, bf16[6,2,3136,128]{3,2,1,0:T(8,128)(2,1)}, s32[6,4]{0,1:T(4,128)S(1)}, bf16[6,2,64,128]{3,2,1,0:T(8,128)(2,1)}, ...), condition=%wide.while_cond.1, body=%wide.while_body.1.sunk | while | flops 16413 | bytes 164043 | solution.py:34
  185.7 55.0 %while.4 = (s32[]{:T(128)}, bf16[6,2,3136,128]{3,2,1,0:T(8,128)(2,1)}, s32[6,4]{0,1:T(4,128)S(1)}, bf16[6,2,64,128]{3,2,1,0:T(8,128)(2,1)}, s32[]{:T(128)}, /*index=5*/s32[4]{0:T(128)S(1)}, s32[]{:T(128)}) while((s32[]{:T(128)}, bf16[6,2,3136,128]{3,2,1,0:T(8,128)(2,1)}, s32[6,4]{0,1:T(4,128)S(1)}, bf16[6,2,64,128]{3,2,1,0:T(8,128)(2,1)}, s32[]{:T(128)}, ...), condition=%wide.while_cond, body=%wide.while_body.sunk | while | flops 16413 | bytes 164043 | solution.py:34
  240.7 27.9 %fusion.150 = (f32[6,2,6,64]{3,2,1,0:T(8,128)S(1)}, bf16[6,2,6,64,3136]{4,3,2,1,0:T(8,128)(2,1)}) fusion(pred[6,64,3136]{2,1,0:T(8,128)(4,1)S(1)} %copy-done.6, bf16[6,2,3136,128]{3,2,1,0:T(8,128)(2,1)} %get-tuple-element.8, bf16[6,2,6,64,64]{4,3,2,1,0:T(8,128)(2,1)} %slice.305, bf16[6,2,6,64,32]{4,3,2,1,0:T(8,128)(2,1)} %get-tuple-element.108, ...), kind=kOutput, calls=%fused_computation.179 | convolution fusion | flops 3775171584 | bytes 40937472 | tf_op jit(solution)/shard_map/sub | solution.py:41
  268.5 16.3 %divide_convert_fusion.1 = bf16[6,2,6,64,128]{4,3,1,2,0:T(8,128)(2,1)S(1)} fusion(bf16[6,2,3136,128]{3,2,1,0:T(8,128)(2,1)} %get-tuple-element.16, bf16[6,2,6,64,3136]{4,3,2,1,0:T(8,128)(2,1)} %get-tuple-element.92, f32[6,2,6,64]{3,1,2,0:T(2,128)S(1)} %copy.36), kind=kOutput, calls=%fused_computation.96 | convolution fusion | flops 3700555776 | bytes 39733248 | tf_op jit(solution)/shard_map/bkgcs,bksh->bkgch/dot_general | solution.py:43
  294.3 34.7 %reduce-scatter.5.cloned.1.call-done = bf16[6,16,4096]{2,1,0:T(8,128)(2,1)} async-done(((bf16[6,64,4096]{2,1,0:T(8,128)(2,1)}), bf16[6,16,4096]{2,1,0:T(8,128)(2,1)}) %reduce-scatter.5.cloned.1.call-update) | async-done | bytes 786448 | tf_op jit(solution)/shard_map/reduce_scatter | solution.py:81
  332.1 25.6 %all-gather.7.cloned.1.call-done = bf16[6,64,4096]{2,1,0:T(8,128)(2,1)} async-done(((bf16[6,16,4096]{2,1,0:T(8,128)(2,1)}), bf16[6,64,4096]{2,1,0:T(8,128)(2,1)}) %all-gather.7.cloned.1.call-update) | async-done | bytes 3145744 | tf_op jit(solution)/shard_map/all_gather | solution.py:84
  357.6 21.1 %fusion.213 = bf16[6,64,4096]{2,1,0:T(8,128)(2,1)} fusion(bf16[2,4096,4096]{2,1,0:T(8,128)(2,1)} %param.20, bf16[6,64,4096]{2,1,0:T(8,128)(2,1)} %all-gather.7.cloned.1.call-done), kind=kOutput, calls=%bitcast_fusion.4.clone.2 | convolution fusion | flops 12889620480 | bytes 39845888 | tf_op jit(solution)/shard_map/bcd,df->bcf/dot_general | solution.py:85
  378.8 21.1 %fusion.54 = bf16[6,64,4096]{2,1,0:T(8,128)(2,1)} fusion(bf16[2,4096,4096]{2,1,0:T(8,128)(2,1)} %param.21, bf16[6,64,4096]{2,1,0:T(8,128)(2,1)} %fusion.213), kind=kOutput, calls=%fused_computation.64 | convolution fusion | flops 12886474752 | bytes 39845888 | tf_op jit(solution)/shard_map/bcf,fd->bcd/dot_general | solution.py:87
  400.0 32.0 %reduce-scatter.7.cloned.1.call-done = bf16[6,16,4096]{2,1,0:T(8,128)(2,1)} async-done(((bf16[6,64,4096]{2,1,0:T(8,128)(2,1)}), bf16[6,16,4096]{2,1,0:T(8,128)(2,1)}) %reduce-scatter.7.cloned.1.call-update) | async-done | bytes 786448 | tf_op jit(solution)/shard_map/reduce_scatter | solution.py:88
  442.2 16.7 %copy.80 = bf16[1,4096,1536]{1,2,0:T(8,128)(2,1)} copy(bf16[1,4096,1536]{2,1,0:T(8,128)(2,1)} %get-tuple-element.95) | data formatting | bytes 25165824
  479.7 54.7 %while.7 = (s32[]{:T(128)}, bf16[6,2,3136,128]{3,2,1,0:T(8,128)(2,1)}, s32[6,4]{0,1:T(4,128)S(1)}, bf16[6,2,64,128]{3,2,1,0:T(8,128)(2,1)}, s32[]{:T(128)}, /*index=5*/s32[4]{0:T(128)S(1)}, s32[]{:T(128)}) while((s32[]{:T(128)}, bf16[6,2,3136,128]{3,2,1,0:T(8,128)(2,1)}, s32[6,4]{0,1:T(4,128)S(1)}, bf16[6,2,64,128]{3,2,1,0:T(8,128)(2,1)}, ...), condition=%wide.while_cond.3, body=%wide.while_body.3.sunk | while | flops 16413 | bytes 164043 | solution.py:34
  535.6 53.6 %while.6 = (s32[]{:T(128)}, bf16[6,2,3136,128]{3,2,1,0:T(8,128)(2,1)}, s32[6,4]{0,1:T(4,128)S(1)}, bf16[6,2,64,128]{3,2,1,0:T(8,128)(2,1)S(1)}, s32[]{:T(128)}, /*index=5*/s32[4]{0:T(128)S(1)}, s32[]{:T(128)}) while((s32[]{:T(128)}, bf16[6,2,3136,128]{3,2,1,0:T(8,128)(2,1)}, s32[6,4]{0,1:T(4,128)S(1)}, bf16[6,2,64,128]{3,2,1,0:T(8,128)(2,1)S(1)}, ...), condition=%wide.while_cond.2, body=%wide.while_body.2.sunk | while | flops 16413 | bytes 164043 | solution.py:34
  589.2 28.0 %fusion.149 = (f32[6,2,6,64]{3,2,1,0:T(8,128)S(1)}, bf16[6,2,6,64,3136]{4,3,2,1,0:T(8,128)(2,1)}) fusion(pred[6,64,3136]{2,1,0:T(8,128)(4,1)} %iota_compare_fusion, bf16[6,2,3136,128]{3,2,1,0:T(8,128)(2,1)} %get-tuple-element.24, bf16[6,2,6,64,64]{4,3,2,1,0:T(8,128)(2,1)} %slice.304, bf16[6,2,6,64,32]{4,3,2,1,0:T(8,128)(2,1)} %get-tuple-element.106, ...), kind=kOutput, calls=%fused_computation.178 | convolution fusion | flops 3775171584 | bytes 40937472 | tf_op jit(solution)/shard_map/sub | solution.py:41
  617.2 16.2 %divide_convert_fusion = bf16[6,2,6,64,128]{4,3,1,2,0:T(8,128)(2,1)S(1)} fusion(bf16[6,2,3136,128]{3,2,1,0:T(8,128)(2,1)} %get-tuple-element.32, bf16[6,2,6,64,3136]{4,3,2,1,0:T(8,128)(2,1)} %get-tuple-element.90, f32[6,2,6,64]{3,1,2,0:T(2,128)S(1)} %copy.46), kind=kOutput, calls=%fused_computation.93 | convolution fusion | flops 3700555776 | bytes 39733248 | tf_op jit(solution)/shard_map/bkgcs,bksh->bkgch/dot_general | solution.py:43
  643.0 31.9 %reduce-scatter.9.cloned.1.call-done = bf16[6,16,4096]{2,1,0:T(8,128)(2,1)} async-done(((bf16[6,64,4096]{2,1,0:T(8,128)(2,1)}), bf16[6,16,4096]{2,1,0:T(8,128)(2,1)}) %reduce-scatter.9.cloned.1.call-update) | async-done | bytes 786448 | tf_op jit(solution)/shard_map/reduce_scatter | solution.py:81
  678.0 25.5 %all-gather.11.cloned.1.call-done = bf16[6,64,4096]{2,1,0:T(8,128)(2,1)} async-done(((bf16[6,16,4096]{2,1,0:T(8,128)(2,1)}), bf16[6,64,4096]{2,1,0:T(8,128)(2,1)}) %all-gather.11.cloned.1.call-update) | async-done | bytes 3145744 | tf_op jit(solution)/shard_map/all_gather | solution.py:84
  703.6 21.1 %fusion.217 = bf16[6,64,4096]{2,1,0:T(8,128)(2,1)} fusion(bf16[2,4096,4096]{2,1,0:T(8,128)(2,1)} %param.20, bf16[6,64,4096]{2,1,0:T(8,128)(2,1)} %all-gather.11.cloned.1.call-done), kind=kOutput, calls=%bitcast_fusion.5.clone.2 | convolution fusion | flops 12889620480 | bytes 39845888 | tf_op jit(solution)/shard_map/bcd,df->bcf/dot_general | solution.py:85
  724.7 21.1 %fusion.57 = bf16[6,64,4096]{2,1,0:T(8,128)(2,1)} fusion(bf16[2,4096,4096]{2,1,0:T(8,128)(2,1)} %param.21, bf16[6,64,4096]{2,1,0:T(8,128)(2,1)} %fusion.217), kind=kOutput, calls=%fused_computation.65 | convolution fusion | flops 12886474752 | bytes 39845888 | tf_op jit(solution)/shard_map/bcf,fd->bcd/dot_general | solution.py:87
  745.9 25.5 %pad_maximum_fusion = (bf16[2,6,2,3136,128]{4,3,2,1,0:T(8,128)(2,1)}, bf16[2,6,2,3136,128]{4,3,2,1,0:T(8,128)(2,1)}) fusion(bf16[1,6,2,3136,128]{4,3,2,1,0:T(8,128)(2,1)} %bitcast.316, bf16[1,6,2,3136,128]{4,3,2,1,0:T(8,128)(2,1)} %bitcast.318, bf16[1,6,2,3136,128]{4,3,2,1,0:T(8,128)(2,1)} %bitcast.317, bf16[1,6,2,3136,128]{4,3,2,1,0:T(8,128)(2,1)} %bitcast.319), kind=kLoop, calls=%fused_computation.42 | loop fusion | flops 19267584 | bytes 77070336 | tf_op jit(solution)/shard_map/stack | solution.py:92
  (243 shorter events, 326.2 us)
Async XLA Ops:
  7.2 8.3 %copy-start.19 = (s32[6]{0:T(128)S(1)}, s32[6]{0:T(128)}, u32[]{:S(2)}) copy-start(s32[6]{0:T(128)} %param.13) | copy-start | bytes 76
  7.2 103.7 %all-gather.5.cloned.1.call-start = ((), (), s32[]{:S(2)}) async-start(), calls=%async_computation.4 | async-start | bytes 3932160 | tf_op jit(solution)/shard_map/all_gather | solution.py:71
  15.4 313.6 %reduce-scatter.5.cloned.1.call-start = ((), (), s32[]{:S(2)}) async-start(), calls=%async_computation.5 | async-start | bytes 3932160 | tf_op jit(solution)/shard_map/reduce_scatter | solution.py:81
  15.5 15.1 %copy-start.2 = (bf16[2,4096,256]{2,1,0:T(8,128)(2,1)S(1)}, bf16[2,4096,256]{2,1,0:T(8,128)(2,1)}, u32[]{:S(2)}) copy-start(bf16[2,4096,256]{2,1,0:T(8,128)(2,1)} %param.18) | copy-start | bytes 12582916
  60.7 16.8 %copy-start.20 = (s32[3]{0:T(128)S(1)}, s32[3]{0:T(128)}, u32[]{:S(2)}) copy-start(s32[3]{0:T(128)} %constant.31.clone.1) | copy-start | bytes 40
  93.2 17.7 %copy-start.4 = (bf16[1,4096,256]{1,2,0:T(8,128)(2,1)S(1)}, bf16[1,4096,256]{1,2,0:T(8,128)(2,1)}, u32[]{:S(2)}) copy-start(bf16[1,4096,256]{1,2,0:T(8,128)(2,1)} %copy.78) | copy-start | bytes 6291460
  125.9 114.7 %copy-start.6 = (pred[6,64,3136]{2,1,0:T(8,128)(4,1)S(1)}, pred[6,64,3136]{2,1,0:T(8,128)(4,1)}, u32[]{:S(2)}) copy-start(pred[6,64,3136]{2,1,0:T(8,128)(4,1)} %iota_compare_fusion) | copy-start | bytes 3612676
  240.6 27.9 %copy-start.7 = (s32[6,4]{0,1:T(4,128)}, s32[6,4]{0,1:T(4,128)S(1)}, u32[]{:S(2)}) copy-start(s32[6,4]{0,1:T(4,128)S(1)} %get-tuple-element.370) | copy-start | bytes 292
  240.7 27.9 %copy-start.11 = (s32[4]{0:T(128)}, s32[4]{0:T(128)S(1)}, u32[]{:S(2)}) copy-start(s32[4]{0:T(128)S(1)} %get-tuple-element.377) | copy-start | bytes 52
  294.0 34.9 %copy-start = (bf16[6,16,4096]{2,1,0:T(8,128)(2,1)S(1)}, bf16[6,16,4096]{2,1,0:T(8,128)(2,1)}, u32[]{:S(2)}) copy-start(bf16[6,16,4096]{2,1,0:T(8,128)(2,1)} %param.12) | copy-start | bytes 2359300
  294.0 36.7 %copy-start.17 = (f32[1,1,4096]{2,1,0:T(1,128)S(1)}, f32[1,1,4096]{2,1,0:T(1,128)}, u32[]{:S(2)}) copy-start(f32[1,1,4096]{2,1,0:T(1,128)} %get-tuple-element.118) | copy-start | bytes 49156
  294.0 36.7 %copy-start.18 = (f32[1,1,4096]{2,1,0:T(1,128)S(1)}, f32[1,1,4096]{2,1,0:T(1,128)}, u32[]{:S(2)}) copy-start(f32[1,1,4096]{2,1,0:T(1,128)} %get-tuple-element.114) | copy-start | bytes 49156
  294.0 63.6 %all-gather.7.cloned.1.call-start = ((), (), s32[]{:S(2)}) async-start(), calls=%async_computation.6 | async-start | bytes 3932160 | tf_op jit(solution)/shard_map/all_gather | solution.py:84
  332.0 100.0 %reduce-scatter.7.cloned.1.call-start = ((), (), s32[]{:S(2)}) async-start(), calls=%async_computation.7 | async-start | bytes 3932160 | tf_op jit(solution)/shard_map/reduce_scatter | solution.py:88
  399.9 33.9 %copy-start.15 = (f32[1,1,4096]{2,1,0:T(1,128)S(1)}, f32[1,1,4096]{2,1,0:T(1,128)}, u32[]{:S(2)}) copy-start(f32[1,1,4096]{2,1,0:T(1,128)} %get-tuple-element.120) | copy-start | bytes 49156
  399.9 33.9 %copy-start.16 = (f32[1,1,4096]{2,1,0:T(1,128)S(1)}, f32[1,1,4096]{2,1,0:T(1,128)}, u32[]{:S(2)}) copy-start(f32[1,1,4096]{2,1,0:T(1,128)} %get-tuple-element.116) | copy-start | bytes 49156
  400.0 60.8 %all-gather.9.cloned.1.call-start = ((), (), s32[]{:S(2)}) async-start(), calls=%async_computation.8 | async-start | bytes 3932160 | tf_op jit(solution)/shard_map/all_gather | solution.py:71
  433.8 5.4 copy-start.1
  435.1 239.8 %reduce-scatter.9.cloned.1.call-start = ((), (), s32[]{:S(2)}) async-start(), calls=%async_computation.9 | async-start | bytes 3932160 | tf_op jit(solution)/shard_map/reduce_scatter | solution.py:81
  478.0 56.5 %copy-start.9 = (bf16[6,2,64,32]{3,2,1,0:T(8,128)(2,1)S(1)}, bf16[6,2,64,32]{3,2,1,0:T(8,128)(2,1)}, u32[]{:S(2)}) copy-start(bf16[6,2,64,32]{3,2,1,0:T(8,128)(2,1)} %get-tuple-element.110) | copy-start | bytes 147460
  642.8 33.9 %copy-start.13 = (f32[1,1,4096]{2,1,0:T(1,128)S(1)}, f32[1,1,4096]{2,1,0:T(1,128)}, u32[]{:S(2)}) copy-start(f32[1,1,4096]{2,1,0:T(1,128)} %get-tuple-element.117) | copy-start | bytes 49156
  642.8 33.9 %copy-start.14 = (f32[1,1,4096]{2,1,0:T(1,128)S(1)}, f32[1,1,4096]{2,1,0:T(1,128)}, u32[]{:S(2)}) copy-start(f32[1,1,4096]{2,1,0:T(1,128)} %get-tuple-element.113) | copy-start | bytes 49156
  642.8 60.8 %all-gather.11.cloned.1.call-start = ((), (), s32[]{:S(2)}) async-start(), calls=%async_computation.10 | async-start | bytes 3932160 | tf_op jit(solution)/shard_map/all_gather | solution.py:84
  678.0 100.0 %reduce-scatter.11.cloned.1.call-start = ((), (), s32[]{:S(2)}) async-start(), calls=%async_computation.11 | async-start | bytes 3932160 | tf_op jit(solution)/shard_map/reduce_scatter | solution.py:88
  (7 other events, 18.0 us)
Sparse Core Ops, SparseCore 0:
  15.5 28.2 all-gather.4
  294.2 34.7 reduce-scatter.4
  332.1 25.4 all-gather.6
  400.1 31.9 reduce-scatter.6
  435.2 25.4 all-gather.8
  642.9 31.9 reduce-scatter.8
  678.1 25.4 all-gather.10
  746.0 31.9 reduce-scatter.10
where the time goes:
time: 802 us; the launch traced here: 787 us
  matrix products  218 us (27%)
  local copies, waits for them, and re-layouts  200 us (25%)
  other arithmetic  195 us (24%)
  waiting for transfers between devices  158 us (20%)
  between operations  14.6 us (2%)
    scatter x48, other arithmetic  140 us
    scatter x72, local copies, waits for them, and re-layouts  79.9 us
    reduce_scatter x2, waiting for transfers between devices, device_fn(): lax.psum_scatter(attn_part, 'tp', scatter_dimension=1, tiled=True)  66.6 us
    sub x2, matrix products, attention(): weights = jnp.exp(scores - peak)  55.8 us
    all_gather x2, waiting for transfers between devices, device_fn(): normed_mlp_all = lax.all_gather(normed_mlp, 'tp', axis=1, tiled=True)  51.1 us
    unnamed x53, local copies, waits for them, and re-layouts  46.4 us
    dot_general x2, matrix products, device_fn(): jnp.einsum('bcf,fd->bcd', act_sq, w_down[layer], preferred_element_type=j...  42.3 us
    dot_general x2, matrix products, device_fn(): jnp.einsum('bcd,df->bcf', normed_mlp_all, w_up[layer], preferred_element_...  42.3 us
  transfers between devices with their start and end apart: 8, of which 7 were waited for; matrix products, arithmetic and copies ran while one was open for 18% of the time, Pallas kernels for 0%

commit v1 on v0

v1 whole, which is shorter than its diff:
```python
import functools
import math

import jax
import jax.numpy as jnp
from jax import lax
from jax.experimental import pallas as pl
from jax.experimental.pallas import tpu as pltpu
from jax.sharding import PartitionSpec as P

LN_EPS = 1e-5
ROPE_BASE = 10000.0
NEG_BIG = -1e30
BF = jnp.bfloat16
F32 = jnp.float32


def layer_norm1p(values_in, gain, bias):
    x_float = values_in.astype(F32)
    row_mean = jnp.mean(x_float, axis=-1, keepdims=True)
    centered = x_float - row_mean
    variance = jnp.mean(centered * centered, axis=-1, keepdims=True)
    normed = centered * lax.rsqrt(variance + LN_EPS)
    return (normed * (1.0 + gain.astype(F32)) + bias.astype(F32)).astype(BF)


def rope_tables(positions, head_dim):
    rot = head_dim // 2
    half = rot // 2
    inv_freq = ROPE_BASE ** (-(jnp.arange(half, dtype=F32) * (2.0 / rot)))
    angles = positions.astype(F32)[:, None] * inv_freq
    cos_a, sin_a = jnp.cos(angles), jnp.sin(angles)
    zero = jnp.zeros_like(sin_a)
    rest = jnp.zeros((positions.shape[0], head_dim - rot), F32)
    c_tab = jnp.concatenate([cos_a, cos_a, rest + 1.0], axis=-1)
    s_up = jnp.concatenate([zero, sin_a, rest], axis=-1)
    s_dn = jnp.concatenate([-sin_a, zero, rest], axis=-1)
    return jnp.stack([c_tab, s_up, s_dn])


def attn_kernel(layer, dims, start_ref, q_ref, k_ref, v_ref, tab_ref, kc_hbm, vc_hbm, *rest):
    kv, group, toks, hd, s_len, ch, n_ch = dims
    if layer > 0:
        rest = rest[2:]
    ctx_ref, ko_hbm, vo_hbm, kbuf, vbuf, sbuf, qbuf, mbuf, lbuf, abuf, in_sem, out_sem = rest
    b = pl.program_id(0)
    nb = pl.num_programs(0)
    slot = lax.rem(b, 2)
    other = 1 - slot
    s_pad = kbuf.shape[2]
    win = toks + 16
    rows = group * toks
    coef = (hd ** -0.5) * math.log2(math.e)

    def load(bb, sl, go):
        for i, (src, dst) in enumerate(((kc_hbm, kbuf), (vc_hbm, vbuf))):
            copy = pltpu.make_async_copy(src.at[layer, bb], dst.at[sl, :, pl.ds(0, s_len), :], in_sem.at[sl, i])
            copy.start() if go else copy.wait()

    def save(bb, sl, go):
        for i, (src, dst) in enumerate(((kbuf, ko_hbm), (vbuf, vo_hbm))):
            copy = pltpu.make_async_copy(src.at[sl, :, pl.ds(0, s_len), :], dst.at[layer, bb], out_sem.at[sl, i])
            copy.start() if go else copy.wait()

    @pl.when(b == 0)
    def _():
        load(b, slot, True)
        if s_pad > s_len:
            for sl in range(2):
                kbuf[sl, :, s_len:, :] = jnp.zeros((kv, s_pad - s_len, hd), BF)
                vbuf[sl, :, s_len:, :] = jnp.zeros((kv, s_pad - s_len, hd), BF)

    @pl.when(b > 0)
    def _():
        save(b - 1, other, False)

    @pl.when(b + 1 < nb)
    def _():
        load(b + 1, other, True)

    c_tab, s_up, s_dn = tab_ref[0], tab_ref[1], tab_ref[2]
    half = hd // 4

    def rope(x):
        return x * c_tab + pltpu.roll(x, half, 1) * s_up + pltpu.roll(x, hd - half, 1) * s_dn

    for h in range(kv):
        for g in range(group):
            j = h * group + g
            qbuf[h, g * toks:(g + 1) * toks, :] = rope(q_ref[:, j * hd:(j + 1) * hd]).astype(BF)

    start = start_ref[b]
    base = jnp.minimum((start // 16) * 16, s_len - win)
    shift = start - base
    base = pl.multiple_of(base, 16)
    row_id = lax.broadcasted_iota(jnp.int32, (win, hd), 0)
    is_new = jnp.logical_and(row_id >= shift, row_id < shift + toks)

    load(b, slot, False)
    for h in range(kv):
        cols = slice(h * hd, (h + 1) * hd)
        for buf, fresh in ((kbuf, rope(k_ref[:, cols])), (vbuf, v_ref[:, cols])):
            fresh = fresh.astype(BF).astype(F32)
            fresh = jnp.concatenate([fresh, jnp.zeros((16, hd), F32)], axis=0)
            fresh = pltpu.roll(fresh, shift, 0)
            old = buf[slot, h, pl.ds(base, win), :].astype(F32)
            buf[slot, h, pl.ds(base, win), :] = jnp.where(is_new, fresh, old).astype(BF)
    save(b, slot, True)

    mbuf[...] = jnp.full(mbuf.shape, NEG_BIG, F32)
    lbuf[...] = jnp.zeros(lbuf.shape, F32)
    abuf[...] = jnp.zeros(abuf.shape, F32)
    n_full = start // ch
    n_used = (start + toks + ch - 1) // ch

    def score_step(masked, j, carry):
        if masked:
            lane = lax.broadcasted_iota(jnp.int32, (rows, ch), 1)
            tok = lax.rem(lax.broadcasted_iota(jnp.int32, (rows, ch), 0), toks)
            ok = lane - tok <= start - j * ch
        for h in range(kv):
            keys = kbuf[slot, h, pl.ds(pl.multiple_of(j * ch, ch), ch), :]
            s = lax.dot_general(qbuf[h], keys, (((1,), (1,)), ((), ())), preferred_element_type=F32)
            if masked:
                s = jnp.where(ok, s, NEG_BIG)
            sbuf[h, j] = s
            peak = mbuf[h]
            for t in range(ch // 128):
                peak = jnp.maximum(peak, s[:, t * 128:(t + 1) * 128])
            mbuf[h] = peak
        return carry

    lax.fori_loop(0, n_full, functools.partial(score_step, False), 0)
    lax.fori_loop(n_full, n_used, functools.partial(score_step, True), 0)
    for h in range(kv):
        mbuf[h] = jnp.broadcast_to(jnp.max(mbuf[h], axis=-1, keepdims=True), (rows, 128))

    def value_step(j, carry):
        for h in range(kv):
            peak = mbuf[h]
            total = lbuf[h]
            parts = []
            for t in range(ch // 128):
                e = jnp.exp2((sbuf[h, j, :, t * 128:(t + 1) * 128] - peak) * coef)
                total = total + e
                parts.append(e.astype(BF))
            lbuf[h] = total
            vals = vbuf[slot, h, pl.ds(pl.multiple_of(j * ch, ch), ch), :]
            abuf[h] += jnp.dot(jnp.concatenate(parts, axis=1), vals, preferred_element_type=F32)
        return carry

    lax.fori_loop(0, n_used, value_step, 0)
    for h in range(kv):
        ctx = (abuf[h] / jnp.sum(lbuf[h], axis=-1, keepdims=True)).astype(BF)
        for g in range(group):
            j = h * group + g
            ctx_ref[:, j * hd:(j + 1) * hd] = ctx[g * toks:(g + 1) * toks, :]

    @pl.when(b == nb - 1)
    def _():
        save(b, slot, False)


def attend(layer, q, k, v, tabs, start_pos, k_cache, v_cache, prev):
    n_seq = start_pos.shape[0]
    _, _, kv, s_len, hd = k_cache.shape
    toks = q.shape[0] // n_seq
    group = q.shape[1] // (kv * hd)
    n_ch = -(-s_len // 640)
    ch = 128 * -(-s_len // (128 * n_ch))
    rows = group * toks
    dims = (kv, group, toks, hd, s_len, ch, n_ch)
    any_spec = pl.BlockSpec(memory_space=pl.ANY)
    row_map = lambda b, *_: (b, 0)
    cache_shape = jax.ShapeDtypeStruct(k_cache.shape, BF)
    args = [start_pos, q, k, v, tabs, k_cache, v_cache] + list(prev)
    return pl.pallas_call(
        functools.partial(attn_kernel, layer, dims),
        grid_spec=pltpu.PrefetchScalarGridSpec(
            num_scalar_prefetch=1,
            grid=(n_seq,),
            in_specs=[
                pl.BlockSpec((toks, q.shape[1]), row_map),
                pl.BlockSpec((toks, kv * hd), row_map),
                pl.BlockSpec((toks, kv * hd), row_map),
                pl.BlockSpec((3, toks, hd), lambda b, *_: (0, b, 0)),
            ] + [any_spec] * (2 + len(prev)),
            out_specs=[pl.BlockSpec((toks, q.shape[1]), row_map), any_spec, any_spec],
            scratch_shapes=[
                pltpu.VMEM((2, kv, ch * n_ch, hd), BF),
                pltpu.VMEM((2, kv, ch * n_ch, hd), BF),
                pltpu.VMEM((kv, n_ch, rows, ch), F32),
                pltpu.VMEM((kv, rows, hd), BF),
                pltpu.VMEM((kv, rows, 128), F32),
                pltpu.VMEM((kv, rows, 128), F32),
                pltpu.VMEM((kv, rows, hd), F32),
                pltpu.SemaphoreType.DMA((2, 2)),
                pltpu.SemaphoreType.DMA((2, 2)),
            ],
        ),
        out_shape=[jax.ShapeDtypeStruct(q.shape, BF), cache_shape, cache_shape],
        input_output_aliases={7: 1, 8: 2} if prev else {},
        compiler_params=pltpu.CompilerParams(vmem_limit_bytes=60 * 1024 * 1024, dimension_semantics=("arbitrary",)),
        cost_estimate=pl.CostEstimate(flops=8_000_000_000, bytes_accessed=80_000_000, transcendentals=15_000_000),
        name="attend",
    )(*args)


def solution(mesh):
    tp_size = mesh.shape['tp']
    tok_spec = P('dp', 'tp', None)
    cache_spec = P(None, 'dp', 'tp', None, None)
    col_spec = P(None, None, 'tp')
    row_spec = P(None, 'tp', None)

    def device_fn(x_loc, start_pos, k_cache, v_cache, w_q, w_k, w_v, w_o, w_up, w_down, ln_gain, ln_bias):
        n_layers = w_q.shape[0]
        n_seq, tok_loc, d_model = x_loc.shape
        new_len = tok_loc * tp_size
        rows = n_seq * new_len
        positions = (start_pos[:, None] + jnp.arange(new_len, dtype=jnp.int32)[None, :]).reshape(rows)
        tabs = rope_tables(positions, k_cache.shape[4])
        hidden = x_loc
        prev = ()
        for layer in range(n_layers):
            normed = layer_norm1p(hidden, ln_gain[layer, 0], ln_bias[layer, 0])
            normed_all = lax.all_gather(normed, 'tp', axis=1, tiled=True).reshape(rows, d_model)
            q_proj = jnp.dot(normed_all, w_q[layer], preferred_element_type=F32)
            k_proj = jnp.dot(normed_all, w_k[layer], preferred_element_type=F32)
            v_proj = jnp.dot(normed_all, w_v[layer], preferred_element_type=F32)
            context, k_out, v_out = attend(layer, q_proj, k_proj, v_proj, tabs, start_pos, k_cache, v_cache, prev)
            prev = (k_out, v_out)
            attn_part = jnp.dot(context, w_o[layer], preferred_element_type=F32).astype(BF)
            attn_part = attn_part.reshape(n_seq, new_len, d_model)
            attn_loc = lax.psum_scatter(attn_part, 'tp', scatter_dimension=1, tiled=True)
            after_attn = (hidden.astype(F32) + attn_loc.astype(F32)).astype(BF)
            normed_mlp = layer_norm1p(after_attn, ln_gain[layer, 1], ln_bias[layer, 1])
            normed_mlp_all = lax.all_gather(normed_mlp, 'tp', axis=1, tiled=True).reshape(rows, d_model)
            up_val = jnp.dot(normed_mlp_all, w_up[layer], preferred_element_type=F32)
            act_sq = jnp.square(jnp.maximum(up_val, 0.0)).astype(BF)
            mlp_part = jnp.dot(act_sq, w_down[layer], preferred_element_type=F32).astype(BF)
            mlp_part = mlp_part.reshape(n_seq, new_len, d_model)
            mlp_loc = lax.psum_scatter(mlp_part, 'tp', scatter_dimension=1, tiled=True)
            hidden = (after_attn.astype(F32) + mlp_loc.astype(F32)).astype(BF)
        return hidden, prev[0], prev[1]

    return jax.shard_map(device_fn, mesh=mesh, in_specs=(tok_spec, P('dp'), cache_spec, cache_spec, col_spec, col_spec, col_spec, row_spec, col_spec, row_spec, P(), P()), out_specs=(tok_spec, cache_spec, cache_spec), check_vma=False)
```

time: 802 us -> 474 us (0.59)
  local copies, waits for them, and re-layouts: 200 us -> 0.27 us
  other arithmetic: 195 us -> 20.3 us
  matrix products: 218 us -> 139 us
  waiting for transfers between devices: 158 us -> 228 us
  Pallas kernels: 0 us -> 62.4 us
    scatter x49 -> x0, other arithmetic: 140 us -> none
    scatter x72 -> x0, local copies, waits for them, and re-layouts: 79.9 us -> none
    pallas_call x0 -> x2, Pallas kernels: none -> 62.4 us  [attend(): pl.pallas_call(functools.partial(attn_kernel, layer, dims), grid_spec=plt...]
    sub x2 -> x0, matrix products: 55.8 us -> none  [attention(): weights = jnp.exp(scores - peak)]
    all_gather x4, waiting for transfers between devices: 52.9 us -> 102 us  [the longest x2 51.4 us: device_fn(): lax.all_gather(normed, 'tp', axis=1, tiled=True).reshape(rows, d_model)]
    unnamed x53 -> x12, local copies, waits for them, and re-layouts: 46.4 us -> 0.02 us
    slice x8 -> x0, local copies, waits for them, and re-layouts: 44 us -> none  [the longest x1 17.7 us: device_fn(): w_o[layer].reshape(kv_loc, group_size, head_dim, d_model)]
    squeeze x2 -> x0, local copies, waits for them, and re-layouts: 30 us -> none  [the longest x1 15.1 us: device_fn(): v_new = jax.vmap(write_rows)(v_cache[layer], v_rows, start_pos)]
  transfers between devices with their start and end apart: 8 -> 8, of which waited for: 7 -> 8; matrix products, arithmetic and copies ran while one was open for 18% -> 0% of each run, Pallas kernels for 0% -> 0%
where the time goes in v1:
time: 474 us; the launch traced here: 466 us
  waiting for transfers between devices  228 us (48%)
  matrix products  139 us (29%)
  Pallas kernels  62.4 us (13%)
  other arithmetic  20.3 us (4%)
  between operations  14.7 us (3%)
    reduce_scatter x2, waiting for transfers between devices, device_fn(): mlp_loc = lax.psum_scatter(mlp_part, 'tp', scatter_dimension=1, tiled=True)  64.1 us
    pallas_call x2, Pallas kernels, attend(): pl.pallas_call(functools.partial(attn_kernel, layer, dims), grid_spec=plt...  62.4 us
    reduce_scatter x2, waiting for transfers between devices, device_fn(): lax.psum_scatter(attn_part, 'tp', scatter_dimension=1, tiled=True)  61.8 us
    all_gather x2, waiting for transfers between devices, device_fn(): lax.all_gather(normed, 'tp', axis=1, tiled=True).reshape(rows, d_model)  51.4 us
    all_gather x2, waiting for transfers between devices, device_fn(): lax.all_gather(normed_mlp, 'tp', axis=1, tiled=True).reshape(rows, d_model)  50.7 us
    dot_general x2, matrix products, device_fn(): up_val = jnp.dot(normed_mlp_all, w_up[layer], preferred_element_type=F32)  42.3 us
    dot_general x2, matrix products, device_fn(): jnp.dot(act_sq, w_down[layer], preferred_element_type=F32).astype(BF)  42.3 us
    dot_general x2, matrix products, device_fn(): jnp.dot(context, w_o[layer], preferred_element_type=F32).astype(BF)  19 us
  transfers between devices with their start and end apart: 8, of which 8 were waited for; matrix products, arithmetic and copies ran while one was open for 0% of the time, Pallas kernels for 0%

profile of v1, /device:TPU:0, one launch (start us, length us, event | category | flops | bytes accessed | tf_op | source)
XLA Modules:
  0.0 465.6 jit_solution(2956765456715266503)
XLA Ops:
  11.8 2.4 fusion.75
  16.5 26.1 %all-gather.5.cloned.1.call-done = bf16[6,64,4096]{2,1,0:T(8,128)(2,1)} async-done(((bf16[6,16,4096]{2,1,0:T(8,128)(2,1)}), bf16[6,64,4096]{2,1,0:T(8,128)(2,1)}) %all-gather.5.cloned.1.call-update) | async-done | bytes 3145744 | tf_op jit(solution)/shard_map/all_gather | solution.py:227
  42.6 4.4 fusion.44.v_ref
  47.0 3.8 fusion.46.k_ref
  50.8 9.4 %fusion.18.q_ref = f32[384,1536]{1,0:T(8,128)} fusion(bf16[384,4096]{1,0:T(8,128)(2,1)S(1)} %bitcast.144, bf16[2,4096,1536]{2,1,0:T(8,128)(2,1)} %param.16), kind=kOutput, calls=%fused_computation.18 | convolution fusion | flops 4831838208 | bytes 18087936 | tf_op jit(solution)/shard_map/dot_general | solution.py:228
  60.2 31.2 %attend.2 = (bf16[384,1536]{1,0:T(8,128)(2,1)}, bf16[2,6,2,3136,128]{4,3,2,1,0:T(8,128)(2,1)}, bf16[2,6,2,3136,128]{4,3,2,1,0:T(8,128)(2,1)}) custom-call(s32[6]{0:T(128)} %start_ref.3, f32[384,1536]{1,0:T(8,128)} %fusion.18.q_ref, f32[384,256]{1,0:T(8,128)} %fusion.46.k_ref, f32[384,256]{1,0:T(8,128)} %fusion.44.v_ref, ...), custom_call_target="tpu_custom_call" | custom-call | flops 8000000000 | bytes 80000000 | tf_op jit(solution)/shard_map/attend/pallas_call | solution.py:177
  91.5 9.5 %fusion.34 = bf16[384,4096]{1,0:T(8,128)(2,1)} fusion(bf16[384,1536]{1,0:T(8,128)(2,1)} %get-tuple-element.9, bf16[2,1536,4096]{2,1,0:T(8,128)(2,1)} %param.19), kind=kOutput, calls=%fused_computation.28 | convolution fusion | flops 4833411072 | bytes 16908288 | tf_op jit(solution)/shard_map/dot_general | solution.py:233
  101.0 30.9 %reduce-scatter.5.cloned.1.call-done = bf16[6,16,4096]{2,1,0:T(8,128)(2,1)} async-done(((bf16[6,64,4096]{2,1,0:T(8,128)(2,1)}), bf16[6,16,4096]{2,1,0:T(8,128)(2,1)}) %reduce-scatter.5.cloned.1.call-update) | async-done | bytes 786448 | tf_op jit(solution)/shard_map/reduce_scatter | solution.py:235
  135.3 25.4 %all-gather.7.cloned.1.call-done = bf16[6,64,4096]{2,1,0:T(8,128)(2,1)} async-done(((bf16[6,16,4096]{2,1,0:T(8,128)(2,1)}), bf16[6,64,4096]{2,1,0:T(8,128)(2,1)}) %all-gather.7.cloned.1.call-update) | async-done | bytes 3145744 | tf_op jit(solution)/shard_map/all_gather | solution.py:238
  160.6 21.2 %fusion.138 = bf16[384,4096]{1,0:T(8,128)(2,1)} fusion(bf16[2,4096,4096]{2,1,0:T(8,128)(2,1)} %param.20, bf16[384,4096]{1,0:T(8,128)(2,1)} %bitcast.148), kind=kOutput, calls=%bitcast_fusion.4.clone.2 | convolution fusion | flops 12889620480 | bytes 39845888 | tf_op jit(solution)/shard_map/dot_general | solution.py:239
  181.8 21.1 %fusion.28 = bf16[384,4096]{1,0:T(8,128)(2,1)} fusion(bf16[2,4096,4096]{2,1,0:T(8,128)(2,1)} %param.21, bf16[384,4096]{1,0:T(8,128)(2,1)} %fusion.138), kind=kOutput, calls=%fused_computation.26 | convolution fusion | flops 12886474752 | bytes 39845888 | tf_op jit(solution)/shard_map/dot_general | solution.py:241
  203.0 32.0 %reduce-scatter.7.cloned.1.call-done = bf16[6,16,4096]{2,1,0:T(8,128)(2,1)} async-done(((bf16[6,64,4096]{2,1,0:T(8,128)(2,1)}), bf16[6,16,4096]{2,1,0:T(8,128)(2,1)}) %reduce-scatter.7.cloned.1.call-update) | async-done | bytes 786448 | tf_op jit(solution)/shard_map/reduce_scatter | solution.py:243
  238.4 25.3 %all-gather.9.cloned.1.call-done = bf16[6,64,4096]{2,1,0:T(8,128)(2,1)} async-done(((bf16[6,16,4096]{2,1,0:T(8,128)(2,1)}), bf16[6,64,4096]{2,1,0:T(8,128)(2,1)}) %all-gather.9.cloned.1.call-update) | async-done | bytes 3145744 | tf_op jit(solution)/shard_map/all_gather | solution.py:227
  263.7 4.4 fusion.40.v_ref
  268.1 3.8 fusion.42.k_ref
  271.9 9.4 %fusion.14.q_ref = f32[384,1536]{1,0:T(8,128)} fusion(bf16[384,4096]{1,0:T(8,128)(2,1)S(1)} %bitcast.147, bf16[2,4096,1536]{2,1,0:T(8,128)(2,1)} %param.16), kind=kOutput, calls=%fused_computation.14 | convolution fusion | flops 4831838208 | bytes 18087936 | tf_op jit(solution)/shard_map/dot_general | solution.py:228
  281.3 31.2 %attend.3 = (bf16[384,1536]{1,0:T(8,128)(2,1)}, bf16[2,6,2,3136,128]{4,3,2,1,0:T(8,128)(2,1)}, bf16[2,6,2,3136,128]{4,3,2,1,0:T(8,128)(2,1)}) custom-call(s32[6]{0:T(128)} %start_ref.3, f32[384,1536]{1,0:T(8,128)} %fusion.14.q_ref, f32[384,256]{1,0:T(8,128)} %fusion.42.k_ref, ...), custom_call_target="tpu_custom_call", output_to_operand_aliasing={{1}: (7, {}), {2}: (8, {})} | custom-call | flops 8000000000 | bytes 80000000 | tf_op jit(solution)/shard_map/attend/pallas_call | solution.py:177
  312.6 9.5 %fusion.37 = bf16[384,4096]{1,0:T(8,128)(2,1)} fusion(bf16[384,1536]{1,0:T(8,128)(2,1)} %get-tuple-element.12, bf16[2,1536,4096]{2,1,0:T(8,128)(2,1)} %param.19), kind=kOutput, calls=%fused_computation.29 | convolution fusion | flops 4833411072 | bytes 16908288 | tf_op jit(solution)/shard_map/dot_general | solution.py:233
  322.1 30.9 %reduce-scatter.9.cloned.1.call-done = bf16[6,16,4096]{2,1,0:T(8,128)(2,1)} async-done(((bf16[6,64,4096]{2,1,0:T(8,128)(2,1)}), bf16[6,16,4096]{2,1,0:T(8,128)(2,1)}) %reduce-scatter.9.cloned.1.call-update) | async-done | bytes 786448 | tf_op jit(solution)/shard_map/reduce_scatter | solution.py:235
  356.4 25.3 %all-gather.11.cloned.1.call-done = bf16[6,64,4096]{2,1,0:T(8,128)(2,1)} async-done(((bf16[6,16,4096]{2,1,0:T(8,128)(2,1)}), bf16[6,64,4096]{2,1,0:T(8,128)(2,1)}) %all-gather.11.cloned.1.call-update) | async-done | bytes 3145744 | tf_op jit(solution)/shard_map/all_gather | solution.py:238
  381.7 21.2 %fusion.142 = bf16[384,4096]{1,0:T(8,128)(2,1)} fusion(bf16[2,4096,4096]{2,1,0:T(8,128)(2,1)} %param.20, bf16[384,4096]{1,0:T(8,128)(2,1)} %bitcast.149), kind=kOutput, calls=%bitcast_fusion.5.clone.2 | convolution fusion | flops 12889620480 | bytes 39845888 | tf_op jit(solution)/shard_map/dot_general | solution.py:239
  402.9 21.1 %fusion.31 = bf16[384,4096]{1,0:T(8,128)(2,1)} fusion(bf16[2,4096,4096]{2,1,0:T(8,128)(2,1)} %param.21, bf16[384,4096]{1,0:T(8,128)(2,1)} %fusion.142), kind=kOutput, calls=%fused_computation.27 | convolution fusion | flops 12886474752 | bytes 39845888 | tf_op jit(solution)/shard_map/dot_general | solution.py:241
  424.0 32.1 %reduce-scatter.11.cloned.1.call-done = bf16[6,16,4096]{2,1,0:T(8,128)(2,1)} async-done(((bf16[6,64,4096]{2,1,0:T(8,128)(2,1)}), bf16[6,16,4096]{2,1,0:T(8,128)(2,1)}) %reduce-scatter.11.cloned.1.call-update) | async-done | bytes 786448 | tf_op jit(solution)/shard_map/reduce_scatter | solution.py:243
  456.1 2.2 fusion.79
  (61 shorter events, 17.1 us)
Async XLA Ops:
  7.2 7.2 %copy-start.1 = (s32[6]{0:T(128)S(1)}, s32[6]{0:T(128)}, u32[]{:S(2)}) copy-start(s32[6]{0:T(128)} %start_ref.3) | copy-start | bytes 76
  7.2 35.4 %all-gather.5.cloned.1.call-start = ((), (), s32[]{:S(2)}) async-start(), calls=%async_computation.4 | async-start | bytes 3932160 | tf_op jit(solution)/shard_map/all_gather | solution.py:227
  14.2 117.8 %reduce-scatter.5.cloned.1.call-start = ((), (), s32[]{:S(2)}) async-start(), calls=%async_computation.5 | async-start | bytes 3932160 | tf_op jit(solution)/shard_map/reduce_scatter | solution.py:235
  42.6 4.4 copy-start.2
  47.0 3.8 copy-start.4
  101.0 31.0 %copy-start = (bf16[6,16,4096]{2,1,0:T(8,128)(2,1)S(1)}, bf16[6,16,4096]{2,1,0:T(8,128)(2,1)}, u32[]{:S(2)}) copy-start(bf16[6,16,4096]{2,1,0:T(8,128)(2,1)} %param.12) | copy-start | bytes 2359300
  101.0 59.6 %all-gather.7.cloned.1.call-start = ((), (), s32[]{:S(2)}) async-start(), calls=%async_computation.6 | async-start | bytes 3932160 | tf_op jit(solution)/shard_map/all_gather | solution.py:238
  135.0 100.0 %reduce-scatter.7.cloned.1.call-start = ((), (), s32[]{:S(2)}) async-start(), calls=%async_computation.7 | async-start | bytes 3932160 | tf_op jit(solution)/shard_map/reduce_scatter | solution.py:243
  203.0 60.8 %all-gather.9.cloned.1.call-start = ((), (), s32[]{:S(2)}) async-start(), calls=%async_computation.8 | async-start | bytes 3932160 | tf_op jit(solution)/shard_map/all_gather | solution.py:227
  238.1 114.9 %reduce-scatter.9.cloned.1.call-start = ((), (), s32[]{:S(2)}) async-start(), calls=%async_computation.9 | async-start | bytes 3932160 | tf_op jit(solution)/shard_map/reduce_scatter | solution.py:235
  263.7 4.4 copy-start.3
  268.1 3.8 copy-start.5
  322.1 59.6 %all-gather.11.cloned.1.call-start = ((), (), s32[]{:S(2)}) async-start(), calls=%async_computation.10 | async-start | bytes 3932160 | tf_op jit(solution)/shard_map/all_gather | solution.py:238
  356.1 100.0 %reduce-scatter.11.cloned.1.call-start = ((), (), s32[]{:S(2)}) async-start(), calls=%async_computation.11 | async-start | bytes 3932160 | tf_op jit(solution)/shard_map/reduce_scatter | solution.py:243
Sparse Core Ops, SparseCore 0:
  14.3 28.2 all-gather.4
  101.1 30.7 reduce-scatter.4
  135.1 25.4 all-gather.6
  203.1 31.9 reduce-scatter.6
  238.2 25.4 all-gather.8
  322.2 30.7 reduce-scatter.8
  356.2 25.4 all-gather.10
  424.2 31.9 reduce-scatter.10

commit v2 on v1

--- a/solution.py
+++ b/solution.py
@@ -13,15 +13,6 @@
 NEG_BIG = -1e30
 BF = jnp.bfloat16
 F32 = jnp.float32
-
-
-def layer_norm1p(values_in, gain, bias):
-    x_float = values_in.astype(F32)
-    row_mean = jnp.mean(x_float, axis=-1, keepdims=True)
-    centered = x_float - row_mean
-    variance = jnp.mean(centered * centered, axis=-1, keepdims=True)
-    normed = centered * lax.rsqrt(variance + LN_EPS)
-    return (normed * (1.0 + gain.astype(F32)) + bias.astype(F32)).astype(BF)
 
 
 def rope_tables(positions, head_dim):
@@ -161,11 +152,13 @@
         save(b, slot, False)
 
 
-def attend(layer, q, k, v, tabs, start_pos, k_cache, v_cache, prev):
+def attend(layer, qkv, tabs, start_pos, k_cache, v_cache, prev):
     n_seq = start_pos.shape[0]
     _, _, kv, s_len, hd = k_cache.shape
-    toks = q.shape[0] // n_seq
-    group = q.shape[1] // (kv * hd)
+    toks = qkv.shape[0] // n_seq
+    kv_width = kv * hd
+    q_width = qkv.shape[1] - 2 * kv_width
+    group = q_width // kv_width
     n_ch = -(-s_len // 640)
     ch = 128 * -(-s_len // (128 * n_ch))
     rows = group * toks
@@ -173,19 +166,19 @@
     any_spec = pl.BlockSpec(memory_space=pl.ANY)
     row_map = lambda b, *_: (b, 0)
     cache_shape = jax.ShapeDtypeStruct(k_cache.shape, BF)
-    args = [start_pos, q, k, v, tabs, k_cache, v_cache] + list(prev)
+    args = [start_pos, qkv, qkv, qkv, tabs, k_cache, v_cache] + list(prev)
     return pl.pallas_call(
         functools.partial(attn_kernel, layer, dims),
         grid_spec=pltpu.PrefetchScalarGridSpec(
             num_scalar_prefetch=1,
             grid=(n_seq,),
             in_specs=[
-                pl.BlockSpec((toks, q.shape[1]), row_map),
-                pl.BlockSpec((toks, kv * hd), row_map),
-                pl.BlockSpec((toks, kv * hd), row_map),
+                pl.BlockSpec((toks, q_width), row_map),
+                pl.BlockSpec((toks, kv_width), lambda b, *_: (b, group)),
+                pl.BlockSpec((toks, kv_width), lambda b, *_: (b, group + 1)),
                 pl.BlockSpec((3, toks, hd), lambda b, *_: (0, b, 0)),
             ] + [any_spec] * (2 + len(prev)),
-            out_specs=[pl.BlockSpec((toks, q.shape[1]), row_map), any_spec, any_spec],
+            out_specs=[pl.BlockSpec((toks, q_width), row_map), any_spec, any_spec],
             scratch_shapes=[
                 pltpu.VMEM((2, kv, ch * n_ch, hd), BF),
                 pltpu.VMEM((2, kv, ch * n_ch, hd), BF),
@@ -198,7 +191,7 @@
                 pltpu.SemaphoreType.DMA((2, 2)),
             ],
         ),
-        out_shape=[jax.ShapeDtypeStruct(q.shape, BF), cache_shape, cache_shape],
+        out_shape=[jax.ShapeDtypeStruct((n_seq * toks, q_width), BF), cache_shape, cache_shape],
         input_output_aliases={7: 1, 8: 2} if prev else {},
         compiler_params=pltpu.CompilerParams(vmem_limit_bytes=60 * 1024 * 1024, dimension_semantics=("arbitrary",)),
         cost_estimate=pl.CostEstimate(flops=8_000_000_000, bytes_accessed=80_000_000, transcendentals=15_000_000),
@@ -206,8 +199,284 @@
     )(*args)
 
 
+STEPS = 8
+
+
+def exchange_kernel(cfg, *args):
+    refs = dict(zip(cfg['names'], args))
+    layer, g_layer, ln_row = cfg['layer'], cfg['g_layer'], cfg['ln_row']
+    scatter, gather = cfg['scatter'], cfg['gather']
+    n_seq, toks, d_model = cfg['n_seq'], cfg['toks'], cfg['d_model']
+    rows = n_seq * toks
+    blk = d_model // STEPS
+    me = lax.axis_index('tp')
+    core = lax.rem(me, 2)
+    partner = me + 1 - 2 * core
+    counter = lax.rem(me + 2, 4)
+    diag = lax.rem(partner + 2, 4)
+    order = (me, partner, counter, diag)
+    wbuf, xbuf = refs['wbuf'], refs['xbuf']
+
+    barrier = pltpu.get_barrier_semaphore()
+    for peer in (partner, counter):
+        pl.semaphore_signal(barrier, inc=1, device_id={'tp': peer}, device_id_type=pl.DeviceIdType.MESH)
+
+    def col(n, width=blk):
+        return pl.ds(pl.multiple_of(n * width, width), width)
+
+    x_copy = pltpu.make_async_copy(refs['x_hbm'], xbuf, refs['x_sem'])
+
+    if scatter:
+        depth = cfg['depth']
+        abuf, w_s = refs['abuf'], refs['w_s']
+        a_copies = [pltpu.make_async_copy(refs['a_hbm'].at[:, order[g]], abuf.at[g], refs['a_sem'].at[g]) for g in range(4)]
+
+        def w_copy(n):
+            return pltpu.make_async_copy(w_s.at[layer, :, col(n)], wbuf.at[pl.ds(0, depth), col(n)], refs['sw_sem'].at[n])
+
+        for g in (2, 3):
+            a_copies[g].start()
+        w_copy(0).start()
+        for g in (0, 1):
+            a_copies[g].start()
+        for n in range(1, STEPS):
+            w_copy(n).start()
+    x_copy.start()
+
+    g_copies = []
+    if gather:
+        if cfg['kind'] == 'up':
+            cut = depth
+            for i, (lo, hi) in enumerate(((cut, d_model), (0, cut))):
+                span = pl.ds(lo, hi - lo)
+                g_copies.append(pltpu.make_async_copy(refs['w_up'].at[g_layer, span, :], wbuf.at[span, :], refs['gw_sem'].at[i]))
+        else:
+            at = 0
+            for i, name in enumerate(('w_q', 'w_k', 'w_v')):
+                width = refs[name].shape[2]
+                g_copies.append(pltpu.make_async_copy(refs[name].at[g_layer], wbuf.at[:, pl.ds(at, width)], refs['gw_sem'].at[i]))
+                at += width
+        if not scatter:
+            for copy in g_copies:
+                copy.start()
+        elif cfg['kind'] == 'up':
+            g_copies[0].start()
+
+    def remote(src, dst, send, recv, peer):
+        return pltpu.make_async_remote_copy(src_ref=src, dst_ref=dst, send_sem=send, recv_sem=recv, device_id={'tp': peer}, device_id_type=pl.DeviceIdType.MESH)
+
+    pl.semaphore_wait(barrier, 2)
+
+    if scatter:
+        dsend, drecv, qsend, qrecv, own = refs['dsend'], refs['drecv'], refs['qsend'], refs['qrecv'], refs['own']
+        part = refs['part']
+
+        def d_copy(n, i):
+            return remote(dsend.at[n, i], drecv.at[n, i], refs['ds_sem'].at[n, i], refs['dr_sem'].at[n, i], partner)
+
+        def q_copy(n):
+            return remote(qsend.at[n], qrecv.at[n], refs['qs_sem'].at[n], refs['qr_sem'].at[n], counter)
+
+        for copy in a_copies:
+            copy.wait()
+
+        def s_step(n, carry):
+            w_copy(n).wait()
+            far = jnp.dot(abuf[2:4].reshape(2 * rows, depth), wbuf[0:depth, col(n)], preferred_element_type=F32)
+            dsend[n, 0] = far[rows:].astype(BF)
+            d_copy(n, 0).start()
+            part[...] = far[:rows]
+            near = jnp.dot(abuf[0:2].reshape(2 * rows, depth), wbuf[0:depth, col(n)], preferred_element_type=F32)
+            dsend[n, 1] = near[rows:].astype(BF)
+            d_copy(n, 1).start()
+            own[n] = near[:rows]
+            d_copy(n, 0).wait_recv()
+            qsend[n] = (part[...] + drecv[n, 0].astype(F32)).astype(BF)
+            q_copy(n).start()
+            return carry
+
+        half = STEPS // 2
+        lax.fori_loop(0, half, s_step, 0)
+        if gather and cfg['kind'] == 'qkv':
+            for copy in g_copies:
+                copy.start()
+        lax.fori_loop(half, STEPS, s_step, 0)
+        if gather and cfg['kind'] == 'up':
+            g_copies[1].start()
+
+    x_copy.wait()
+    total = jnp.zeros((rows, 128), F32)
+    for n in range(STEPS):
+        cols = slice(n * blk, (n + 1) * blk)
+        if scatter:
+            d_copy(n, 1).wait_recv()
+            q_copy(n).wait_recv()
+            summed = own[n] + drecv[n, 1].astype(F32) + qrecv[n].astype(F32)
+            fresh = (xbuf[:, cols].astype(F32) + summed.astype(BF).astype(F32)).astype(BF)
+            xbuf[:, cols] = fresh
+        else:
+            fresh = xbuf[:, cols]
+        fresh = fresh.astype(F32)
+        for j in range(blk // 128):
+            total = total + fresh[:, j * 128:(j + 1) * 128]
+    if scatter:
+        out_copy = pltpu.make_async_copy(xbuf, refs['x_out'], refs['x_sem'])
+        out_copy.start()
+
+    if gather:
+        near_h, far_h, acc, stage, y_out = refs['near_h'], refs['far_h'], refs['acc'], refs['stage'], refs['y_out']
+        n_out = acc.shape[1]
+        mean = jnp.sum(total, axis=-1, keepdims=True) / d_model
+        total = jnp.zeros((rows, 128), F32)
+        for n in range(STEPS):
+            diff = xbuf[:, n * blk:(n + 1) * blk].astype(F32) - mean
+            diff = diff * diff
+            for j in range(blk // 128):
+                total = total + diff[:, j * 128:(j + 1) * 128]
+        inv = lax.rsqrt(jnp.sum(total, axis=-1, keepdims=True) / d_model + LN_EPS)
+
+        def c_copy(k):
+            return remote(near_h.at[pl.ds(0, rows), col(k)], far_h.at[pl.ds(0, rows), col(k)], refs['cs_sem'].at[k], refs['cr_sem'].at[k], counter)
+
+        def f_copy(k):
+            return remote(far_h.at[pl.ds(0, rows), col(k)], far_h.at[pl.ds(rows, rows), col(k)], refs['fs_sem'].at[k], refs['fr_sem'].at[k], partner)
+
+        def p_copy(k):
+            return remote(near_h.at[pl.ds(0, rows), col(k)], near_h.at[pl.ds(rows, rows), col(k)], refs['ps_sem'].at[k], refs['pr_sem'].at[k], partner)
+
+        for k in range(STEPS):
+            cols = slice(k * blk, (k + 1) * blk)
+            gain = refs['ln_gain'][ln_row:ln_row + 1, cols].astype(F32)
+            bias = refs['ln_bias'][ln_row:ln_row + 1, cols].astype(F32)
+            normed = (xbuf[:, cols].astype(F32) - mean) * inv
+            near_h[0:rows, cols] = (normed * (1.0 + gain) + bias).astype(BF)
+            if k:
+                c_copy(k - 1).start()
+                p_copy(k - 1).start()
+        acc[...] = jnp.zeros(acc.shape, F32)
+        c_copy(STEPS - 1).start()
+        p_copy(STEPS - 1).start()
+
+        for copy in g_copies:
+            copy.wait()
+        for k in range(STEPS):
+            p_copy(k).wait_recv()
+
+        def finish(value):
+            if cfg['kind'] == 'up':
+                value = jnp.square(jnp.maximum(value, 0.0)).astype(BF)
+            return value.reshape(2, n_seq, toks, value.shape[-1])
+
+        n_blk = n_out // STEPS
+
+        def y_copy(g, n):
+            return pltpu.make_async_copy(stage.at[g, :, :, col(n, n_blk)], y_out.at[:, order[g], :, col(n, n_blk)], refs['y_sem'].at[g, n])
+
+        piece = min(1024, n_out)
+
+        def far_dot(k, cols):
+            return jnp.dot(far_h[:, col(k)], wbuf[col(k), cols], preferred_element_type=F32)
+
+        def near_step(i):
+            near = jnp.dot(near_h[...], wbuf[:, col(i, n_blk)], preferred_element_type=F32)
+            stage[0:2, :, :, col(i, n_blk)] = finish(near)
+            y_copy(0, i).start()
+            y_copy(1, i).start()
+            c_copy(i).wait_recv()
+            f_copy(i).start()
+
+        def g_step(i, carry):
+            near_step(i)
+            f_copy(i - 1).wait_recv()
+            for n in range(n_out // piece):
+                cols = slice(n * piece, (n + 1) * piece)
+                acc[:, cols] += far_dot(i - 1, cols)
+            return carry
+
+        near_step(0)
+        lax.fori_loop(1, STEPS, g_step, 0)
+        f_copy(STEPS - 1).wait_recv()
+        for n in range(n_out // piece):
+            cols = slice(n * piece, (n + 1) * piece)
+            stage[2:4, :, :, cols] = finish(acc[:, cols] + far_dot(STEPS - 1, cols))
+            for m in range(n * piece // n_blk, (n + 1) * piece // n_blk):
+                y_copy(2, m).start()
+                y_copy(3, m).start()
+        for k in range(STEPS):
+            c_copy(k).wait_send()
+            p_copy(k).wait_send()
+            f_copy(k).wait_send()
+            for g in range(4):
+                y_copy(g, k).wait()
+
+    if scatter:
+        for n in range(STEPS):
+            d_copy(n, 0).wait_send()
+            d_copy(n, 1).wait_send()
+            q_copy(n).wait_send()
+        out_copy.wait()
+
+
+def exchange(cid, x, ln_gain, ln_bias, *, n_seq, layer=0, a=None, w_s=None, g_layer=0, ln_row=0, kind=None, weights=()):
+    rows, d_model = x.shape
+    toks = rows // n_seq
+    blk = d_model // STEPS
+    scatter, gather = a is not None, kind is not None
+    any_spec, vmem = pl.BlockSpec(memory_space=pl.ANY), pl.BlockSpec(memory_space=pltpu.VMEM)
+    dma = pltpu.SemaphoreType.DMA
+    ins, outs, scr = [('x_hbm', x, any_spec)], [], []
+    flops, moved = 0, 4_000_000
+    scr += [('wbuf', None), ('xbuf', pltpu.VMEM((rows, d_model), BF)), ('x_sem', dma)]
+    width = 0
+    if scatter:
+        depth = a.shape[3]
+        ins += [('a_hbm', a, any_spec), ('w_s', w_s, any_spec)]
+        outs += [('x_out', jax.ShapeDtypeStruct(x.shape, BF))]
+        scr += [
+            ('abuf', pltpu.VMEM((4, n_seq, toks, depth), BF)), ('a_sem', dma((4,))), ('sw_sem', dma((STEPS,))),
+            ('dsend', pltpu.VMEM((STEPS, 2, rows, blk), BF)), ('drecv', pltpu.VMEM((STEPS, 2, rows, blk), BF)),
+            ('qsend', pltpu.VMEM((STEPS, rows, blk), BF)), ('qrecv', pltpu.VMEM((STEPS, rows, blk), BF)),
+            ('own', pltpu.VMEM((STEPS, rows, blk), F32)), ('part', pltpu.VMEM((rows, blk), F32)),
+            ('ds_sem', dma((STEPS, 2))), ('dr_sem', dma((STEPS, 2))), ('qs_sem', dma((STEPS,))), ('qr_sem', dma((STEPS,))),
+        ]
+        width = d_model
+        w_rows = depth
+        flops += 2 * 4 * rows * depth * d_model
+        moved += depth * d_model * 2
+    if gather:
+        names = ('w_up',) if kind == 'up' else ('w_q', 'w_k', 'w_v')
+        ins += list(zip(names, weights, [any_spec] * len(names)))
+        ins += [('ln_gain', ln_gain, vmem), ('ln_bias', ln_bias, vmem)]
+        n_out = sum(w.shape[2] for w in weights)
+        y_type = BF if kind == 'up' else F32
+        outs += [('y_out', jax.ShapeDtypeStruct((n_seq, 4, toks, n_out), y_type))]
+        scr += [
+            ('near_h', pltpu.VMEM((2 * rows, d_model), BF)), ('far_h', pltpu.VMEM((2 * rows, d_model), BF)),
+            ('acc', pltpu.VMEM((2 * rows, n_out), F32)), ('stage', pltpu.VMEM((4, n_seq, toks, n_out), y_type)),
+            ('gw_sem', dma((3,))), ('y_sem', dma((4, STEPS))),
+        ] + [(s, dma((STEPS,))) for s in ('cs_sem', 'cr_sem', 'fs_sem', 'fr_sem', 'ps_sem', 'pr_sem')]
+        width = max(width, n_out)
+        w_rows = d_model
+        flops += 2 * 4 * rows * n_out * d_model
+        moved += n_out * d_model * 2
+    scr[0] = ('wbuf', pltpu.VMEM((w_rows, width), BF))
+    cfg = dict(
+        names=[i[0] for i in ins] + [o[0] for o in outs] + [s[0] for s in scr], layer=layer, g_layer=g_layer, ln_row=ln_row,
+        scatter=scatter, gather=gather, n_seq=n_seq, toks=toks, d_model=d_model, kind=kind, depth=depth if scatter else 0,
+    )
+    return pl.pallas_call(
+        functools.partial(exchange_kernel, cfg),
+        in_specs=[i[2] for i in ins],
+        out_specs=[any_spec] * len(outs),
+        out_shape=[o[1] for o in outs],
+        scratch_shapes=[s[1] for s in scr],
+        compiler_params=pltpu.CompilerParams(collective_id=cid, has_side_effects=True, vmem_limit_bytes=66_000_000),
+        cost_estimate=pl.CostEstimate(flops=flops, bytes_accessed=moved, transcendentals=0),
+        name=('scatter_' if scatter else '') + ('gather_' + kind if gather else 'end'),
+    )(*[i[1] for i in ins])
+
+
 def solution(mesh):
-    tp_size = mesh.shape['tp']
     tok_spec = P('dp', 'tp', None)
     cache_spec = P(None, 'dp', 'tp', None, None)
     col_spec = P(None, None, 'tp')
@@ -216,32 +485,22 @@
     def device_fn(x_loc, start_pos, k_cache, v_cache, w_q, w_k, w_v, w_o, w_up, w_down, ln_gain, ln_bias):
         n_layers = w_q.shape[0]
         n_seq, tok_loc, d_model = x_loc.shape
-        new_len = tok_loc * tp_size
+        new_len = tok_loc * 4
         rows = n_seq * new_len
         positions = (start_pos[:, None] + jnp.arange(new_len, dtype=jnp.int32)[None, :]).reshape(rows)
         tabs = rope_tables(positions, k_cache.shape[4])
-        hidden = x_loc
+        gain, bias = ln_gain.reshape(2 * n_layers, d_model), ln_bias.reshape(2 * n_layers, d_model)
+        hidden = x_loc.reshape(n_seq * tok_loc, d_model)
         prev = ()
+        qkv, = exchange(0, hidden, gain, bias, n_seq=n_seq, kind='qkv', weights=(w_q, w_k, w_v))
         for layer in range(n_layers):
-            normed = layer_norm1p(hidden, ln_gain[layer, 0], ln_bias[layer, 0])
-            normed_all = lax.all_gather(normed, 'tp', axis=1, tiled=True).reshape(rows, d_model)
-            q_proj = jnp.dot(normed_all, w_q[layer], preferred_element_type=F32)
-            k_proj = jnp.dot(normed_all, w_k[layer], preferred_element_type=F32)
-            v_proj = jnp.dot(normed_all, w_v[layer], preferred_element_type=F32)
-            context, k_out, v_out = attend(layer, q_proj, k_proj, v_proj, tabs, start_pos, k_cache, v_cache, prev)
-            prev = (k_out, v_out)
-            attn_part = jnp.dot(context, w_o[layer], preferred_element_type=F32).astype(BF)
-            attn_part = attn_part.reshape(n_seq, new_len, d_model)
-            attn_loc = lax.psum_scatter(attn_part, 'tp', scatter_dimension=1, tiled=True)
-            after_attn = (hidden.astype(F32) + attn_loc.astype(F32)).astype(BF)
-            normed_mlp = layer_norm1p(after_attn, ln_gain[layer, 1], ln_bias[layer, 1])
-            normed_mlp_all = lax.all_gather(normed_mlp, 'tp', axis=1, tiled=True).reshape(rows, d_model)
-            up_val = jnp.dot(normed_mlp_all, w_up[layer], preferred_element_type=F32)
-            act_sq = jnp.square(jnp.maximum(up_val, 0.0)).astype(BF)
-            mlp_part = jnp.dot(act_sq, w_down[layer], preferred_element_type=F32).astype(BF)
-            mlp_part = mlp_part.reshape(n_seq, new_len, d_model)
-            mlp_loc = lax.psum_scatter(mlp_part, 'tp', scatter_dimension=1, tiled=True)
-            hidden = (after_attn.astype(F32) + mlp_loc.astype(F32)).astype(BF)
-        return hidden, prev[0], prev[1]
+            context, *prev = attend(layer, qkv.reshape(rows, -1), tabs, start_pos, k_cache, v_cache, prev)
+            context = context.reshape(n_seq, 4, tok_loc, -1)
+            hidden, act = exchange(2 * layer + 1, hidden, gain, bias, n_seq=n_seq, layer=layer, a=context, w_s=w_o, g_layer=layer, ln_row=2 * layer + 1, kind='up', weights=(w_up,))
+            if layer + 1 < n_layers:
+                hidden, qkv = exchange(2 * layer + 2, hidden, gain, bias, n_seq=n_seq, layer=layer, a=act, w_s=w_down, g_layer=layer + 1, ln_row=2 * layer + 2, kind='qkv', weights=(w_q, w_k, w_v))
+            else:
+                hidden, = exchange(2 * layer + 2, hidden, gain, bias, n_seq=n_seq, layer=layer, a=act, w_s=w_down)
+        return hidden.reshape(x_loc.shape), prev[0], prev[1]
 
     return jax.shard_map(device_fn, mesh=mesh, in_specs=(tok_spec, P('dp'), cache_spec, cache_spec, col_spec, col_spec, col_spec, row_spec, col_spec, row_spec, P(), P()), out_specs=(tok_spec, cache_spec, cache_spec), check_vma=False)

time: 474 us -> 294 us (0.62); the launches traced: 466 us -> 292 us
  waiting for transfers between devices: 228 us -> 0 us
  Pallas kernels: 62.4 us -> 284 us
  matrix products: 139 us -> 0 us
  other arithmetic: 20.3 us -> 2.58 us
  between operations: 14.7 us -> 0.72 us
  local copies, waits for them, and re-layouts: 0.27 us -> 5.09 us
    pallas_call x0 -> x5, Pallas kernels: none -> 220 us  [exchange(): pl.pallas_call(functools.partial(exchange_kernel, cfg), in_specs=[i[2] fo...]
    dot_general x12 -> x0, matrix products: 139 us -> none  [the longest x2 42.3 us: device_fn(): up_val = jnp.dot(normed_mlp_all, w_up[layer], preferred_element_type=F32)]
    reduce_scatter x4 -> x0, waiting for transfers between devices: 126 us -> none  [the longest x2 64.1 us: device_fn(): mlp_loc = lax.psum_scatter(mlp_part, 'tp', scatter_dimension=1, tiled=True)]
    all_gather x4 -> x0, waiting for transfers between devices: 102 us -> none  [the longest x2 51.4 us: device_fn(): lax.all_gather(normed, 'tp', axis=1, tiled=True).reshape(rows, d_model)]
    convert_element_type x5 -> x0, other arithmetic: 8.39 us -> none  [the longest x4 6.18 us: layer_norm1p(): return (normed * (1.0 + gain.astype(F32)) + bias.astype(F32)).astype(BF)]
    reduce_sum x8 -> x0, other arithmetic: 8.08 us -> none  [the longest x4 5.59 us: layer_norm1p(): row_mean = jnp.mean(x_float, axis=-1, keepdims=True)]
  transfers between devices with their start and end apart: 8 -> 0, of which waited for: 8 -> 0; matrix products, arithmetic and copies ran while one was open for 0% -> 0% of each run, Pallas kernels for 0% -> 0%
where the time goes in v2:
time: 294 us; the launch traced here: 292 us
  Pallas kernels  284 us (97%)
  local copies, waits for them, and re-layouts  5.09 us (2%)
    pallas_call x5, Pallas kernels, exchange(): pl.pallas_call(functools.partial(exchange_kernel, cfg), in_specs=[i[2] fo...  220 us
    pallas_call x2, Pallas kernels, attend(): pl.pallas_call(functools.partial(attn_kernel, layer, dims), grid_spec=plt...  64.2 us

profile of v2, /device:TPU:0, one launch (start us, length us, event | category | flops | bytes accessed | tf_op | source)
XLA Modules:
  0.0 292.5 jit_solution(17354725154746844287)
XLA Ops:
  0.6 0.1 pad.11.clone
  0.7 0.1 pad.8.clone
  0.8 0.7 add_convert_fusion
  1.5 0.1 convert_element_type.11
  1.6 1.4 reshape.53.args_4_.args_6_
  3.0 1.4 reshape.54.args_5_.args_7_
  4.4 0.8 multiply_cosine_fusion
  5.2 0.2 maximum_bitcast_fusion.1
  5.4 0.9 pad_maximum_fusion.tab_ref
  6.3 31.5 %gather_qkv.1 = f32[6,4,16,2048]{3,2,1,0:T(8,128)} custom-call(bf16[96,4096]{1,0:T(8,128)(2,1)} %bitcast.19, bf16[2,4096,1536]{2,1,0:T(8,128)(2,1)} %args_3_.9, bf16[2,4096,256]{2,1,0:T(8,128)(2,1)} %args_4_.4, bf16[2,4096,256]{2,1,0:T(8,128)(2,1)} %args_5_.4, bf16[4,4096]{1,0:T(4,128)(2,1)} %reshape.53.args_4_.args_6_, bf16[4,4096]{1,0:T(4,128)(2,1)} %reshape.54.args_5_.args_7_), custom_call_target="tpu_custom_call" | custom-call | flops 6442450944 | bytes 20777216 | tf_op jit(solution)/shard_map/gather_qkv/pallas_call | solution.py:467
  37.8 32.1 %attend.2 = (bf16[384,1536]{1,0:T(8,128)(2,1)}, bf16[2,6,2,3136,128]{4,3,2,1,0:T(8,128)(2,1)}, bf16[2,6,2,3136,128]{4,3,2,1,0:T(8,128)(2,1)}) custom-call(s32[6]{0:T(128)} %start_ref.3, f32[384,2048]{1,0:T(8,128)} %bitcast.12, f32[384,2048]{1,0:T(8,128)} %bitcast.13, f32[384,2048]{1,0:T(8,128)} %bitcast.14, f32[3,384,128]{2,1,0:T(8,128)} %pad_maximum_fusion.tab_ref, ...), custom_call_target="tpu_custom_call" | custom-call | flops 8000000000 | bytes 80000000 | tf_op jit(solution)/shard_map/attend/pallas_call | solution.py:170
  69.9 50.8 %scatter_gather_up.2 = (bf16[96,4096]{1,0:T(8,128)(2,1)}, bf16[6,4,16,4096]{3,2,1,0:T(8,128)(2,1)}) custom-call(bf16[96,4096]{1,0:T(8,128)(2,1)} %bitcast.20, bf16[6,4,16,1536]{3,2,1,0:T(8,128)(2,1)} %bitcast.22, bf16[2,1536,4096]{2,1,0:T(8,128)(2,1)} %args_2_.11, bf16[2,4096,4096]{2,1,0:T(8,128)(2,1)} %args_3_.10, bf16[4,4096]{1,0:T(4,128)(2,1)} %reshape.53.args_4_.args_6_, ...), custom_call_target="tpu_custom_call" | custom-call | flops 17716740096 | bytes 50137344 | tf_op jit(solution)/shard_map/scatter_gather_up/pallas_call | solution.py:467
  120.7 56.0 %scatter_gather_qkv.1 = (bf16[96,4096]{1,0:T(8,128)(2,1)}, f32[6,4,16,2048]{3,2,1,0:T(8,128)}) custom-call(bf16[96,4096]{1,0:T(8,128)(2,1)} %get-tuple-element.16.args_0_, bf16[6,4,16,4096]{3,2,1,0:T(8,128)(2,1)} %get-tuple-element.17.args_1_, bf16[2,4096,4096]{2,1,0:T(8,128)(2,1)} %args_2_.12, bf16[2,4096,1536]{2,1,0:T(8,128)(2,1)} %args_3_.9, ...), custom_call_target="tpu_custom_call" | custom-call | flops 19327352832 | bytes 54331648 | tf_op jit(solution)/shard_map/scatter_gather_qkv/pallas_call | solution.py:467
  176.8 32.1 %attend.3 = (bf16[384,1536]{1,0:T(8,128)(2,1)}, bf16[2,6,2,3136,128]{4,3,2,1,0:T(8,128)(2,1)}, bf16[2,6,2,3136,128]{4,3,2,1,0:T(8,128)(2,1)}) custom-call(s32[6]{0:T(128)} %start_ref.3, f32[384,2048]{1,0:T(8,128)} %bitcast.15, f32[384,2048]{1,0:T(8,128)} %bitcast.16, f32[384,2048]{1,0:T(8,128)} %bitcast.17, ...), custom_call_target="tpu_custom_call", output_to_operand_aliasing={{1}: (7, {}), {2}: (8, {})} | custom-call | flops 8000000000 | bytes 80000000 | tf_op jit(solution)/shard_map/attend/pallas_call | solution.py:170
  208.9 51.1 %scatter_gather_up.3 = (bf16[96,4096]{1,0:T(8,128)(2,1)}, bf16[6,4,16,4096]{3,2,1,0:T(8,128)(2,1)}) custom-call(bf16[96,4096]{1,0:T(8,128)(2,1)} %get-tuple-element.18.args_0_, bf16[6,4,16,1536]{3,2,1,0:T(8,128)(2,1)} %bitcast.21, bf16[2,1536,4096]{2,1,0:T(8,128)(2,1)} %args_2_.11, bf16[2,4096,4096]{2,1,0:T(8,128)(2,1)} %args_3_.10, ...), custom_call_target="tpu_custom_call" | custom-call | flops 17716740096 | bytes 50137344 | tf_op jit(solution)/shard_map/scatter_gather_up/pallas_call | solution.py:467
  260.0 30.5 %scatter_end.1 = bf16[96,4096]{1,0:T(8,128)(2,1)} custom-call(bf16[96,4096]{1,0:T(8,128)(2,1)} %get-tuple-element.23.args_0_, bf16[6,4,16,4096]{3,2,1,0:T(8,128)(2,1)} %get-tuple-element.24.args_1_, bf16[2,4096,4096]{2,1,0:T(8,128)(2,1)} %args_2_.12), custom_call_target="tpu_custom_call" | custom-call | flops 12884901888 | bytes 37554432 | tf_op jit(solution)/shard_map/scatter_end/pallas_call | solution.py:467
  290.4 2.1 copy.20
  (4 shorter events, 0.0 us)
